TPU v7x, 32 devices: a whole 2x2x4 slice. The times are simulated.
32 devices in a mesh: blk: 8 (over z, core), grp: 4 (over y, x).
Axes of the slice: x: 2, y: 2, z: 4, core: 2. Of those that a mesh axis runs over, the one named last changes fastest.
Arguments:
- images: bfloat16 [4, 2048, 1152], P('grp', 'blk'), may hold values from -1 to 1
- texts: bfloat16 [4, 2048, 1152], P('grp', 'blk'), may hold values from -1 to 1
- labels: int32 [4, 8, 256], P('grp', 'blk'), may hold values from 0 to 255, each once within a row
- partners: int32 [2, 8], replicated, may hold values from 0 to 7, as said below
- logit_scale: float32 [], replicated, may hold values from 1 to 3
- logit_bias: float32 [], replicated, may hold values from -3 to -1
Outputs:
- image_grad: float32 [4, 2048, 1152], P('grp', 'blk')
- text_grad: float32 [4, 2048, 1152], P('grp', 'blk')
- loss: float32 [], replicated
Inputs may be any that keep to these rules, and one draw needn't show every extreme that they name: Each block's labels are a permutation of its 256 text rows. partners[r, i] is block i's partner in round r: partners[r, partners[r, i]] == i and partners[r, i] != i; no two rounds pair the same two blocks.
All inputs are finite; a program needn't handle non-finite values.
Results may differ from a plain program's by a relative error of at most 0.00035.
The roundings to bfloat16 on the way count: a program that leaves them out, or rounds other values in their place, can miss the bound.
Values may be sent and summed in bfloat16 or wider, within the bound.
A program may use at most 64 MiB of HBM per device.

v0:
```python
import jax
import jax.numpy as jnp
from jax import lax
from jax.sharding import PartitionSpec as P


def block_weights(image_rows, text_rows, positive, logit_scale, logit_bias):
    logits = (
        logit_scale * jnp.dot(image_rows, text_rows.T, preferred_element_type=jnp.float32)
        + logit_bias
    )
    signed = jnp.where(positive, jnp.float32(1.0), jnp.float32(-1.0))
    loss_sum = jnp.sum(jax.nn.softplus(-signed * logits))
    weight = (-signed * jax.nn.sigmoid(-signed * logits)).astype(jnp.bfloat16)
    return (loss_sum, weight)


def regroup(received, partner_row):
    row_count, width = received.shape
    devices = partner_row.shape[0]
    pieces = received.reshape(row_count, devices, width // devices)
    pieces = jnp.take(pieces, partner_row, axis=1)
    return pieces.reshape(row_count, width)


def body(images, texts, labels, partners, logit_scale, logit_bias):
    own_images = images[0]
    own_texts = texts[0]
    row_count = own_images.shape[0]
    columns = jnp.arange(row_count, dtype=jnp.int32)
    positive = labels[0, 0][:, None] == columns[None, :]
    nothing = jnp.zeros((row_count, row_count), dtype=bool)
    loss_sum, weight = block_weights(own_images, own_texts, positive, logit_scale, logit_bias)
    image_grad = logit_scale * jnp.dot(weight, own_texts, preferred_element_type=jnp.float32)
    text_grad = logit_scale * jnp.dot(weight.T, own_images, preferred_element_type=jnp.float32)
    for round_index in range(partners.shape[0]):
        partner_row = partners[round_index]
        spread_images, spread_texts = (
            lax.all_to_all(own_images, "blk", split_axis=1, concat_axis=1, tiled=True),
            lax.all_to_all(own_texts, "blk", split_axis=1, concat_axis=1, tiled=True),
        )
        their_images, their_texts = (
            lax.all_to_all(
                regroup(spread_images, partner_row), "blk", split_axis=1, concat_axis=1, tiled=True
            ),
            lax.all_to_all(
                regroup(spread_texts, partner_row), "blk", split_axis=1, concat_axis=1, tiled=True
            ),
        )
        round_loss, weight = block_weights(
            own_images, their_texts, nothing, logit_scale, logit_bias
        )
        image_grad = image_grad + logit_scale * jnp.dot(
            weight, their_texts, preferred_element_type=jnp.float32
        )
        mirror_loss, mirror = block_weights(
            their_images, own_texts, nothing, logit_scale, logit_bias
        )
        text_grad = text_grad + logit_scale * jnp.dot(
            mirror.T, their_images, preferred_element_type=jnp.float32
        )
        loss_sum = loss_sum + round_loss
    loss_all = lax.psum(loss_sum, ("blk", "grp"))
    image_count = lax.axis_size("blk") * lax.axis_size("grp") * row_count
    loss = loss_all / jnp.float32(image_count)
    return (image_grad[None], text_grad[None], loss)


def solution(mesh):
    in_specs = (P("grp", "blk", None), P("grp", "blk", None), P("grp", "blk", None), P(), P(), P())
    out_specs = (P("grp", "blk", None), P("grp", "blk", None), P())
    return jax.shard_map(body, mesh=mesh, in_specs=in_specs, out_specs=out_specs, check_vma=False)
```

profile of v0, /device:TPU:0, one launch (start us, length us, event | category | flops | bytes accessed | tf_op | source)
XLA Modules:
  0.0 164.6 jit_solution(17377873898539275789)
XLA Ops:
  0.6 0.0 copy-start.1
  0.6 2.2 %copy.13 = bf16[1,256,1152]{1,2,0:T(8,128)(2,1)} copy(bf16[1,256,1152]{2,1,0:T(8,128)(2,1)} %param.9) | data formatting | bytes 1179648 | tf_op args[1]
  2.8 6.4 %all-to-all-start = ((bf16[256,8,144]{0,2,1:T(8,128)(2,1)}), bf16[256,8,144]{0,2,1:T(8,128)(2,1)S(1)}, u32[]{:S(2)}, u32[]{:S(2)}) async-start(bf16[256,8,144]{0,2,1:T(8,128)(2,1)} %bitcast.4), calls=%async_computation | async-start | bytes 1179648 | tf_op jit(solution)/shard_map/all_to_all | solution.py:40
  9.2 0.0 copy-done.1
  9.2 0.0 copy-start.6
  9.2 1.1 copy.17
  10.3 15.7 %all-to-all-done = bf16[256,8,144]{0,2,1:T(8,128)(2,1)S(1)} async-done(((bf16[256,8,144]{0,2,1:T(8,128)(2,1)}), bf16[256,8,144]{0,2,1:T(8,128)(2,1)S(1)}, u32[]{:S(2)}, u32[]{:S(2)}) %all-to-all-start) | async-done | bytes 589856 | tf_op jit(solution)/shard_map/all_to_all | solution.py:40
  25.9 3.5 %all-to-all-start.3 = ((bf16[256,8,144]{0,2,1:T(8,128)(2,1)}), bf16[256,8,144]{0,2,1:T(8,128)(2,1)S(1)}, u32[]{:S(2)}, u32[]{:S(2)}) async-start(bf16[256,8,144]{0,2,1:T(8,128)(2,1)} %bitcast.13), calls=%async_computation.3 | async-start | bytes 1179648 | tf_op jit(solution)/shard_map/all_to_all | solution.py:39
  29.5 0.0 copy-done.6
  29.5 0.6 gather_fusion
  30.1 16.0 %all-to-all-done.3 = bf16[256,8,144]{0,2,1:T(8,128)(2,1)S(1)} async-done(((bf16[256,8,144]{0,2,1:T(8,128)(2,1)}), bf16[256,8,144]{0,2,1:T(8,128)(2,1)S(1)}, u32[]{:S(2)}, u32[]{:S(2)}) %all-to-all-start.3) | async-done | bytes 589856 | tf_op jit(solution)/shard_map/all_to_all | solution.py:39
  46.1 0.6 gather_fusion.2
  46.7 1.2 select_bitcast_fusion.1
  47.9 3.5 %all-to-all-start.1 = ((bf16[256,8,144]{0,2,1:T(8,128)(2,1)}), bf16[256,8,144]{0,2,1:T(8,128)(2,1)S(1)}, u32[]{:S(2)}, u32[]{:S(2)}) async-start(bf16[256,8,144]{0,2,1:T(8,128)(2,1)} %get-tuple-element.13), calls=%async_computation.1 | async-start | bytes 1179648 | tf_op jit(solution)/shard_map/all_to_all | solution.py:46
  51.4 0.6 gather_fusion.1
  52.0 0.6 gather_fusion.3
  52.6 1.2 select_bitcast_fusion
  53.8 14.3 %all-to-all-done.1 = bf16[256,8,144]{0,2,1:T(8,128)(2,1)S(1)} async-done(((bf16[256,8,144]{0,2,1:T(8,128)(2,1)}), bf16[256,8,144]{0,2,1:T(8,128)(2,1)S(1)}, u32[]{:S(2)}, u32[]{:S(2)}) %all-to-all-start.1) | async-done | bytes 589856 | tf_op jit(solution)/shard_map/all_to_all | solution.py:46
  68.1 0.0 copy-start.2
  68.1 0.0 copy-start
  68.1 0.0 copy-start.5
  68.1 3.7 %all-to-all-start.2 = ((bf16[256,8,144]{0,2,1:T(8,128)(2,1)}), bf16[256,8,144]{0,2,1:T(8,128)(2,1)S(1)}, u32[]{:S(2)}, u32[]{:S(2)}) async-start(bf16[256,8,144]{0,2,1:T(8,128)(2,1)} %get-tuple-element.11), calls=%async_computation.2 | async-start | bytes 1179648 | tf_op jit(solution)/shard_map/all_to_all | solution.py:46
  73.1 15.4 %all-to-all-done.2 = bf16[256,8,144]{0,2,1:T(8,128)(2,1)S(1)} async-done(((bf16[256,8,144]{0,2,1:T(8,128)(2,1)}), bf16[256,8,144]{0,2,1:T(8,128)(2,1)S(1)}, u32[]{:S(2)}, u32[]{:S(2)}) %all-to-all-start.2) | async-done | bytes 589856 | tf_op jit(solution)/shard_map/all_to_all | solution.py:46
  88.4 0.0 copy-done.2
  88.4 3.5 %all-to-all-start.4 = ((bf16[256,8,144]{0,2,1:T(8,128)(2,1)}), bf16[256,8,144]{0,2,1:T(8,128)(2,1)S(1)}, u32[]{:S(2)}, u32[]{:S(2)}) async-start(bf16[256,8,144]{0,2,1:T(8,128)(2,1)} %get-tuple-element.12), calls=%async_computation.4 | async-start | bytes 1179648 | tf_op jit(solution)/shard_map/all_to_all | solution.py:43
  92.0 0.0 copy-done
  92.0 0.0 copy-done.5
  92.0 1.1 fusion.33
  93.1 0.0 copy-start.4
  93.1 0.7 copy-done.4
  93.8 0.4 fusion.25
  94.2 1.1 fusion.14
  95.3 1.8 %copy.16 = f32[256,256]{0,1:T(8,128)} copy(f32[256,256]{1,0:T(8,128)} %fusion.14) | data formatting | bytes 524288 | tf_op jit(solution)/shard_map/add | solution.py:9
  97.1 2.9 %fusion.34 = (f32[]{:T(128)}, f32[256,256]{0,1:T(8,128)}) fusion(f32[]{:T(128)S(6)} %copy.23, bf16[256,1152]{0,1:T(8,128)(2,1)} %bitcast.91, bf16[1,256,1152]{2,1,0:T(8,128)(2,1)S(1)} %copy-done.1, f32[]{:T(128)S(6)} %copy.22), kind=kOutput, calls=%fused_computation.52 | convolution fusion | flops 151584768 | bytes 1441804 | tf_op jit(solution)/shard_map/dot_general | solution.py:9
  101.4 1.7 %fusion.35 = f32[]{:T(128)} fusion(f32[256,256]{0,1:T(8,128)} %copy.16), kind=kLoop, calls=%fused_computation.53 | loop fusion | flops 458751 | bytes 262148 | tf_op jit(solution)/shard_map/reduce_sum | solution.py:13
  103.7 4.9 %all-to-all-done.4 = bf16[256,8,144]{0,2,1:T(8,128)(2,1)S(1)} async-done(((bf16[256,8,144]{0,2,1:T(8,128)(2,1)}), bf16[256,8,144]{0,2,1:T(8,128)(2,1)S(1)}, u32[]{:S(2)}, u32[]{:S(2)}) %all-to-all-start.4) | async-done | bytes 589856 | tf_op jit(solution)/shard_map/all_to_all | solution.py:43
  108.6 3.5 %all-to-all-start.5 = ((bf16[256,8,144]{0,2,1:T(8,128)(2,1)}), bf16[256,8,144]{0,2,1:T(8,128)(2,1)S(1)}, u32[]{:S(2)}, u32[]{:S(2)}) async-start(bf16[256,8,144]{0,2,1:T(8,128)(2,1)} %get-tuple-element.10), calls=%async_computation.5 | async-start | bytes 1179648 | tf_op jit(solution)/shard_map/all_to_all | solution.py:43
  112.2 2.6 %fusion.28 = f32[256,1152]{1,0:T(8,128)} fusion(bf16[1,256,1152]{2,1,0:T(8,128)(2,1)} %param.8, f32[256,256]{1,0:T(8,128)} %copy-done.4, s32[256]{0:T(256)S(1)} %bitcast.95), kind=kOutput, calls=%fused_computation.42 | convolution fusion | flops 151519232 | bytes 2032640 | tf_op jit(solution)/shard_map/dot_general | solution.py:35
  114.8 40.6 %psum.7 = f32[]{:T(128)} all-reduce(f32[]{:T(128)S(6)} %add.97), channel_id=1, replica_groups=mesh['blk'=8,'grp'=4] {'blk','grp'}, use_global_device_ids=true, to_apply=%region_3.5 | all-reduce | flops 1 | bytes 8 | tf_op jit(solution)/shard_map/psum | solution.py:63
  156.1 0.0 copy-start.3
  156.1 1.6 convolution_add_fusion.3
  157.7 0.0 copy-done.3
  157.7 1.4 fusion.3
  159.1 2.3 %convolution_add_fusion.1 = f32[256,1152]{1,0:T(8,128)S(1)} fusion(f32[256,1152]{1,0:T(8,128)} %fusion.28, bf16[256,1152]{0,1:T(8,128)(2,1)S(1)} %bitcast.87, bf16[1,256,1152]{2,1,0:T(8,128)(2,1)S(1)} %copy-done, f32[]{:T(128)S(6)} %copy.23, f32[]{:T(128)S(6)} %copy.22), kind=kOutput, calls=%fused_computation.5 | convolution fusion | flops 302678016 | bytes 3538952 | tf_op jit(solution)/shard_map/dot_general | solution.py:59
  161.4 0.0 all-to-all-done.5
  161.4 2.0 %fusion.2 = f32[1,256,1152]{2,1,0:T(8,128)} fusion(f32[256,1152]{1,0:T(8,128)S(1)} %convolution_add_fusion.1, bf16[256,1152]{0,1:T(8,128)(2,1)S(1)} %bitcast.88, bf16[1,256,1152]{2,1,0:T(8,128)(2,1)S(1)} %copy-done, f32[]{:T(128)S(6)} %copy.22, f32[]{:T(128)S(6)} %copy.23), kind=kOutput, calls=%fused_computation.10 | convolution fusion | flops 302972928 | bytes 3538952 | tf_op jit(solution)/shard_map/dot_general | solution.py:59
  (3 shorter events, 0.0 us)
Async XLA Ops:
  0.6 8.6 %copy-start.1 = (bf16[1,256,1152]{2,1,0:T(8,128)(2,1)S(1)}, bf16[1,256,1152]{2,1,0:T(8,128)(2,1)}, u32[]{:S(2)}) copy-start(bf16[1,256,1152]{2,1,0:T(8,128)(2,1)} %param.8) | copy-start | bytes 1769476
  2.8 23.1 %all-to-all-start = ((bf16[256,8,144]{0,2,1:T(8,128)(2,1)}), bf16[256,8,144]{0,2,1:T(8,128)(2,1)S(1)}, u32[]{:S(2)}, u32[]{:S(2)}) async-start(bf16[256,8,144]{0,2,1:T(8,128)(2,1)} %bitcast.4), calls=%async_computation | async-start | bytes 1179648 | tf_op jit(solution)/shard_map/all_to_all | solution.py:40
  9.2 20.3 %copy-start.6 = (s32[2,8]{1,0:T(2,128)S(1)}, s32[2,8]{1,0:T(2,128)}, u32[]{:S(2)}) copy-start(s32[2,8]{1,0:T(2,128)} %param.11) | copy-start | bytes 196
  25.9 20.2 %all-to-all-start.3 = ((bf16[256,8,144]{0,2,1:T(8,128)(2,1)}), bf16[256,8,144]{0,2,1:T(8,128)(2,1)S(1)}, u32[]{:S(2)}, u32[]{:S(2)}) async-start(bf16[256,8,144]{0,2,1:T(8,128)(2,1)} %bitcast.13), calls=%async_computation.3 | async-start | bytes 1179648 | tf_op jit(solution)/shard_map/all_to_all | solution.py:39
  47.9 20.2 %all-to-all-start.1 = ((bf16[256,8,144]{0,2,1:T(8,128)(2,1)}), bf16[256,8,144]{0,2,1:T(8,128)(2,1)S(1)}, u32[]{:S(2)}, u32[]{:S(2)}) async-start(bf16[256,8,144]{0,2,1:T(8,128)(2,1)} %get-tuple-element.13), calls=%async_computation.1 | async-start | bytes 1179648 | tf_op jit(solution)/shard_map/all_to_all | solution.py:46
  68.1 20.3 %copy-start.2 = (bf16[256,8,144]{0,2,1:T(8,128)(2,1)}, bf16[256,8,144]{0,2,1:T(8,128)(2,1)S(1)}, u32[]{:S(2)}) copy-start(bf16[256,8,144]{0,2,1:T(8,128)(2,1)S(1)} %all-to-all-done.1) | copy-start | bytes 1769476
  68.1 23.9 %copy-start = (bf16[1,256,1152]{2,1,0:T(8,128)(2,1)S(1)}, bf16[1,256,1152]{2,1,0:T(8,128)(2,1)}, u32[]{:S(2)}) copy-start(bf16[1,256,1152]{2,1,0:T(8,128)(2,1)} %param.9) | copy-start | bytes 1769476
  68.1 23.9 %copy-start.5 = (s32[1,1,256]{2,1,0:T(1,128)S(1)}, s32[1,1,256]{2,1,0:T(1,128)}, u32[]{:S(2)}) copy-start(s32[1,1,256]{2,1,0:T(1,128)} %param.10) | copy-start | bytes 3076
  68.1 20.3 %all-to-all-start.2 = ((bf16[256,8,144]{0,2,1:T(8,128)(2,1)}), bf16[256,8,144]{0,2,1:T(8,128)(2,1)S(1)}, u32[]{:S(2)}, u32[]{:S(2)}) async-start(bf16[256,8,144]{0,2,1:T(8,128)(2,1)} %get-tuple-element.11), calls=%async_computation.2 | async-start | bytes 1179648 | tf_op jit(solution)/shard_map/all_to_all | solution.py:46
  88.4 20.2 %all-to-all-start.4 = ((bf16[256,8,144]{0,2,1:T(8,128)(2,1)}), bf16[256,8,144]{0,2,1:T(8,128)(2,1)S(1)}, u32[]{:S(2)}, u32[]{:S(2)}) async-start(bf16[256,8,144]{0,2,1:T(8,128)(2,1)} %get-tuple-element.12), calls=%async_computation.4 | async-start | bytes 1179648 | tf_op jit(solution)/shard_map/all_to_all | solution.py:43
  93.1 0.7 copy-start.4
  108.6 52.8 %all-to-all-start.5 = ((bf16[256,8,144]{0,2,1:T(8,128)(2,1)}), bf16[256,8,144]{0,2,1:T(8,128)(2,1)S(1)}, u32[]{:S(2)}, u32[]{:S(2)}) async-start(bf16[256,8,144]{0,2,1:T(8,128)(2,1)} %get-tuple-element.10), calls=%async_computation.5 | async-start | bytes 1179648 | tf_op jit(solution)/shard_map/all_to_all | solution.py:43
  156.1 1.6 copy-start.3
where the time goes:
time: 166 us; the launch traced here: 165 us
  waiting for transfers between devices  66.2 us (40%)
  blocking collectives  40.6 us (24%)
  starting transfers between devices  24.2 us (15%)
  matrix products  15.5 us (9%)
  local copies, waits for them, and re-layouts  8.11 us (5%)
  between operations  5.84 us (4%)
  other arithmetic  4.12 us (2%)
    psum x1, blocking collectives, body(): loss_all = lax.psum(loss_sum, ('blk', 'grp'))  40.6 us
    all_to_all x2, waiting for transfers between devices, body(): lax.all_to_all(regroup(spread_texts, partner_row), 'blk', split_axis=1, c...  29.6 us
    all_to_all x1, waiting for transfers between devices, body(): lax.all_to_all(own_images, 'blk', split_axis=1, concat_axis=1, tiled=True)  16 us
    all_to_all x1, waiting for transfers between devices, body(): lax.all_to_all(own_texts, 'blk', split_axis=1, concat_axis=1, tiled=True)  15.7 us
    all_to_all x2, starting transfers between devices, body(): lax.all_to_all(regroup(spread_texts, partner_row), 'blk', split_axis=1, c...  7.21 us
    all_to_all x2, starting transfers between devices, body(): lax.all_to_all(regroup(spread_images, partner_row), 'blk', split_axis=1,...  7.08 us
    all_to_all x1, starting transfers between devices, body(): lax.all_to_all(own_texts, 'blk', split_axis=1, concat_axis=1, tiled=True)  6.35 us
    dot_general x3, matrix products, block_weights(): jnp.dot(image_rows, text_rows.T, preferred_element_type=jnp.float32)  5.17 us
  transfers between devices with their start and end apart: 6, of which 5 were waited for; matrix products, arithmetic and copies ran while one was open for 13% of the time, Pallas kernels for 0%

commit v1 on v0

--- a/solution.py
+++ b/solution.py
@@ -1,7 +1,15 @@
+import functools
 import jax
 import jax.numpy as jnp
 from jax import lax
+from jax.experimental import pallas as pl
+from jax.experimental.pallas import tpu as pltpu
 from jax.sharding import PartitionSpec as P
+
+MESH = pl.DeviceIdType.MESH
+CHUNK_ROWS = 32
+VMEM_BUDGET = 48 * 1024 * 1024
+VMEM_LIMIT = 60 * 1024 * 1024
 
 
 def block_weights(image_rows, text_rows, positive, logit_scale, logit_bias):
@@ -23,7 +31,7 @@
     return pieces.reshape(row_count, width)
 
 
-def body(images, texts, labels, partners, logit_scale, logit_bias):
+def spread_body(images, texts, labels, partners, logit_scale, logit_bias):
     own_images = images[0]
     own_texts = texts[0]
     row_count = own_images.shape[0]
@@ -53,7 +61,7 @@
         image_grad = image_grad + logit_scale * jnp.dot(
             weight, their_texts, preferred_element_type=jnp.float32
         )
-        mirror_loss, mirror = block_weights(
+        _, mirror = block_weights(
             their_images, own_texts, nothing, logit_scale, logit_bias
         )
         text_grad = text_grad + logit_scale * jnp.dot(
@@ -66,7 +74,281 @@
     return (image_grad[None], text_grad[None], loss)
 
 
+def logistic_terms(value):
+    small = jnp.exp(-jnp.abs(value))
+    inverse = 1.0 / (1.0 + small)
+    weight = jnp.where(value >= 0, inverse, small * inverse)
+    return weight, jnp.maximum(value, 0.0) + jnp.log1p(small)
+
+
+def rows_dot(rows, own):
+    return lax.dot_general(rows, own, (((1,), (1,)), ((), ())), preferred_element_type=jnp.float32)
+
+
+def weight_dot(weight, rows):
+    return lax.dot_general(
+        weight, rows, (((0,), (0,)), ((), ())), preferred_element_type=jnp.float32
+    )
+
+
+def fold(terms):
+    rows, columns = terms.shape
+    total = jnp.sum(terms.reshape(rows // 8, 8, columns), axis=0)
+    return sum(total[:, c : c + 128] for c in range(0, columns, 128))
+
+
+def exchange_kernel(
+    n, groups, rounds, edges,
+    partners_ref, scale_ref, bias_ref, labels_ref, images_ref, texts_ref,
+    image_acc, text_acc, loss_ref,
+    own, loss_sum, group_loss, block_loss,
+    own_sem, load_sem, recv_sem, send_sem, slot_sem,
+    group_send, group_recv, block_send, block_recv, *buffers,
+):
+    chunks = len(edges) - 1
+    held, slots = buffers[:chunks], buffers[chunks:]
+    chips = n // 2
+    me = lax.axis_index("blk")
+    grp = lax.axis_index("grp")
+    chip = lax.div(me, 2)
+    core = lax.rem(me, 2)
+    sibling = me + 1 - 2 * core
+    inner = jnp.logical_and(chip > 0, chip < chips - 1)
+    outer = jnp.logical_not(inner)
+    up_all = chip < chips - 2
+    down_all = chip > 1
+    beside_end = jnp.logical_or(chip == 1, chip == chips - 2)
+    end_device = jnp.where(chip == 1, me - 2, me + 2)
+    scale = scale_ref[0]
+    bias = bias_ref[0]
+
+    loads = []
+    for k in range(chunks):
+        part = pl.ds(edges[k], edges[k + 1] - edges[k])
+        loads.append([
+            pltpu.make_async_copy(ref.at[0, part], held[k].at[me, i], load_sem.at[k, i])
+            for i, ref in enumerate((images_ref, texts_ref))
+        ])
+        for copy in loads[-1]:
+            copy.start()
+    own_loads = [
+        pltpu.make_async_copy(ref.at[0], own.at[i], own_sem.at[i])
+        for i, ref in enumerate((images_ref, texts_ref))
+    ]
+    for copy in own_loads:
+        copy.start()
+
+    barrier = pltpu.get_barrier_semaphore()
+    for step in range(1, n):
+        pl.semaphore_signal(
+            barrier, inc=1, device_id={"blk": lax.rem(me + step, n)}, device_id_type=MESH
+        )
+    for step in range(1, groups):
+        pl.semaphore_signal(
+            barrier, inc=1, device_id={"grp": lax.rem(grp + step, groups)}, device_id_type=MESH
+        )
+    pl.semaphore_wait(barrier, n - 1 + groups - 1)
+
+    pending = []
+
+    def copy_of(k, entry, way, target):
+        return pltpu.make_async_remote_copy(
+            src_ref=held[k].at[entry],
+            dst_ref=held[k].at[entry],
+            send_sem=send_sem.at[k, way, lax.div(entry, 2)],
+            recv_sem=recv_sem.at[k, entry],
+            device_id={"blk": target},
+            device_id_type=MESH,
+        )
+
+    def send(k, entry, way, target, when):
+        pending.append((when, lambda: copy_of(k, entry, way, target).wait_send()))
+        pl.when(when)(lambda: copy_of(k, entry, way, target).start())
+
+    def arrived(k, entry, when):
+        pl.when(when)(lambda: copy_of(k, entry, 0, sibling).wait_recv())
+
+    def send_own(k, when):
+        send(k, me, 0, me + 2, jnp.logical_and(when, up_all))
+        send(k, me, 1, me - 2, jnp.logical_and(when, down_all))
+        send(k, me, 2, sibling, jnp.logical_and(when, inner))
+
+    def relay(k, passing):
+        for distance in range(1, chips - 1):
+            below = jnp.logical_and(inner, chip >= distance)
+            below = jnp.logical_and(below, up_all == passing)
+            arrived(k, me - 2 * distance, below)
+            if passing:
+                send(k, me - 2 * distance, 0, me + 2, below)
+            send(k, me - 2 * distance, 2, sibling, below)
+            above = jnp.logical_and(inner, chip + distance < chips)
+            above = jnp.logical_and(above, down_all == passing)
+            arrived(k, me + 2 * distance, above)
+            if passing:
+                send(k, me + 2 * distance, 1, me - 2, above)
+            send(k, me + 2 * distance, 2, sibling, above)
+
+    def slot_copy(k):
+        return pltpu.make_async_remote_copy(
+            src_ref=slots[k],
+            dst_ref=held[k].at[pl.ds(n, rounds)],
+            send_sem=slot_sem.at[k],
+            recv_sem=recv_sem.at[k, n],
+            device_id={"blk": end_device},
+            device_id_type=MESH,
+        )
+
+    def select(k):
+        for at in range(chips):
+            arrived(k, 2 * at + 1 - core, inner)
+
+        @pl.when(beside_end)
+        def _():
+            for r in range(rounds):
+                slots[k][r] = held[k][partners_ref[r, end_device]]
+            slot_copy(k).start()
+
+        pl.when(outer)(lambda: slot_copy(k).wait_recv())
+
+    def compute(k):
+        found = [
+            held[k][jnp.where(inner, partners_ref[r, me], n + r)] for r in range(rounds)
+        ]
+        their_images = jnp.concatenate([rows[0] for rows in found], axis=0)
+        their_texts = jnp.concatenate([rows[1] for rows in found], axis=0)
+        weight, terms = logistic_terms(scale * rows_dot(their_texts, own[0]) + bias)
+        loss_sum[...] += fold(terms)
+        mirror, _ = logistic_terms(scale * rows_dot(their_images, own[1]) + bias)
+        image_acc[0] += weight_dot(weight.astype(jnp.bfloat16), their_texts)
+        text_acc[0] += weight_dot(mirror.astype(jnp.bfloat16), their_images)
+
+    always = me >= 0
+    for k in range(chunks):
+        for copy in loads[k]:
+            copy.wait()
+        send_own(k, always if k < 2 else outer)
+
+    for copy in own_loads:
+        copy.wait()
+    logits = scale * rows_dot(own[1], own[0]) + bias
+    positive = lax.broadcasted_iota(jnp.int32, logits.shape, 0) == labels_ref[0]
+    signed = jnp.where(positive, -1.0, 1.0)
+    weight, terms = logistic_terms(signed * logits)
+    weight = (signed * weight).astype(jnp.bfloat16)
+    loss_sum[...] = fold(terms)
+    image_acc[0] = weight_dot(weight, own[1])
+    text_acc[0] = jnp.dot(weight, own[0], preferred_element_type=jnp.float32)
+
+    relay(0, True)
+    for k in range(chunks):
+        if k + 1 < chunks:
+            relay(k + 1, True)
+        if k + 2 < chunks:
+            send_own(k + 2, inner)
+        relay(k, False)
+        select(k)
+        compute(k)
+
+    def share(slot, position, count, axis, send, recv):
+        def copy(step):
+            return pltpu.make_async_remote_copy(
+                src_ref=slot.at[position],
+                dst_ref=slot.at[position],
+                send_sem=send.at[step],
+                recv_sem=recv.at[position],
+                device_id={axis: lax.rem(position + step, count)},
+                device_id_type=MESH,
+            )
+
+        for step in range(1, count):
+            copy(step).start()
+        for step in range(1, count):
+            other = lax.rem(position + step, count)
+            pltpu.make_async_remote_copy(
+                src_ref=slot.at[other],
+                dst_ref=slot.at[other],
+                send_sem=send.at[step],
+                recv_sem=recv.at[other],
+                device_id={axis: other},
+                device_id_type=MESH,
+            ).wait_recv()
+        for step in range(1, count):
+            copy(step).wait_send()
+        total = slot[0]
+        for at in range(1, count):
+            total = total + slot[at]
+        return total
+
+    group_loss[grp] = loss_sum[...]
+    block_loss[me] = share(group_loss, grp, groups, "grp", group_send, group_recv)
+    total = share(block_loss, me, n, "blk", block_send, block_recv)
+    loss_ref[0, 0] = jnp.sum(total) / jnp.float32(n * groups * own.shape[1])
+
+    for when, wait in pending:
+        pl.when(when)(wait)
+    for k in range(chunks):
+        pl.when(beside_end)(lambda k=k: slot_copy(k).wait_send())
+
+
+def chunk_edges(rows):
+    return list(range(0, rows, CHUNK_ROWS)) + [rows]
+
+
+def gather_body(n, groups, images, texts, labels, partners, logit_scale, logit_bias):
+    _, rows, width = images.shape
+    rounds = partners.shape[0]
+    edges = chunk_edges(rows)
+    chunks = len(edges) - 1
+    sizes = [edges[k + 1] - edges[k] for k in range(chunks)]
+    vmem = pl.BlockSpec(memory_space=pltpu.VMEM)
+    smem = pl.BlockSpec(memory_space=pltpu.SMEM)
+    hbm = pl.BlockSpec(memory_space=pl.ANY)
+    dma = pltpu.SemaphoreType.DMA
+    grad = jax.ShapeDtypeStruct(images.shape, jnp.float32)
+    image_grad, text_grad, loss = pl.pallas_call(
+        functools.partial(exchange_kernel, n, groups, rounds, edges),
+        out_shape=(grad, grad, jax.ShapeDtypeStruct((1, 1), jnp.float32)),
+        in_specs=[smem, smem, smem, vmem, hbm, hbm],
+        out_specs=(vmem, vmem, smem),
+        scratch_shapes=[
+            pltpu.VMEM((2, rows, width), images.dtype),
+            pltpu.VMEM((8, 128), jnp.float32),
+            pltpu.VMEM((groups, 8, 128), jnp.float32),
+            pltpu.VMEM((n, 8, 128), jnp.float32),
+            dma((2,)),
+            dma((chunks, 2)),
+            dma((chunks, n + 1)),
+            dma((chunks, 3, n // 2)),
+            dma((chunks,)),
+            dma((groups,)),
+            dma((groups,)),
+            dma((n,)),
+            dma((n,)),
+        ]
+        + [pltpu.VMEM((n + rounds, 2, size, width), images.dtype) for size in sizes]
+        + [pltpu.VMEM((rounds, 2, size, width), images.dtype) for size in sizes],
+        compiler_params=pltpu.CompilerParams(
+            collective_id=0, has_side_effects=True, vmem_limit_bytes=VMEM_LIMIT
+        ),
+    )(partners, logit_scale.reshape(1), logit_bias.reshape(1), labels, images, texts)
+    return logit_scale * image_grad, logit_scale * text_grad, loss.reshape(())
+
+
 def solution(mesh):
     in_specs = (P("grp", "blk", None), P("grp", "blk", None), P("grp", "blk", None), P(), P(), P())
     out_specs = (P("grp", "blk", None), P("grp", "blk", None), P())
+    n, groups = mesh.shape["blk"], mesh.shape["grp"]
+
+    def body(images, texts, labels, partners, logit_scale, logit_bias):
+        _, rows, width = images.shape
+        rounds = partners.shape[0]
+        block = 2 * rows * width * images.dtype.itemsize
+        needed = block * (n + 2 * rounds + 1) + 2 * rows * width * 4
+        fits = needed <= VMEM_BUDGET and n % 2 == 0 and n >= 8
+        if fits and rows % CHUNK_ROWS == 0 and rows % 128 == 0 and width % 128 == 0:
+            return gather_body(
+                n, groups, images, texts, labels, partners, logit_scale, logit_bias
+            )
+        return spread_body(images, texts, labels, partners, logit_scale, logit_bias)
+
     return jax.shard_map(body, mesh=mesh, in_specs=in_specs, out_specs=out_specs, check_vma=False)

time: 166 us -> 89.6 us (0.54)
  Pallas kernels: 0 us -> 82.4 us
  waiting for transfers between devices: 66.2 us -> 0 us
  blocking collectives: 40.6 us -> 0 us
  starting transfers between devices: 24.2 us -> 0 us
  matrix products: 15.5 us -> 0 us
  local copies, waits for them, and re-layouts: 8.11 us -> 0 us
  between operations: 5.84 us -> 3.75 us
    pallas_call x0 -> x1, Pallas kernels: none -> 82.4 us  [gather_body(): pl.pallas_call(functools.partial(exchange_kernel, n, groups, rounds, edge...]
    all_to_all x6 -> x0, waiting for transfers between devices: 66.2 us -> none  [the longest x2 29.6 us: body(): lax.all_to_all(regroup(spread_texts, partner_row), 'blk', split_axis=1, c...]
    psum x1 -> x0, blocking collectives: 40.6 us -> none  [body(): loss_all = lax.psum(loss_sum, ('blk', 'grp'))]
    all_to_all x6 -> x0, starting transfers between devices: 24.2 us -> none  [the longest x2 7.21 us: body(): lax.all_to_all(regroup(spread_texts, partner_row), 'blk', split_axis=1, c...]
    dot_general x9 -> x0, matrix products: 15.5 us -> none  [the longest x3 5.17 us: block_weights(): jnp.dot(image_rows, text_rows.T, preferred_element_type=jnp.float32)]
    unnamed x16 -> x0, local copies, waits for them, and re-layouts: 3.98 us -> none
    mul x0 -> x1, other arithmetic: none -> 3.18 us  [gather_body(): return (logit_scale * image_grad, logit_scale * text_grad, loss.reshape(()))]
    select_n x2 -> x0, other arithmetic: 2.39 us -> none  [regroup(): pieces = jnp.take(pieces, partner_row, axis=1)]
  transfers between devices with their start and end apart: 6 -> 0, of which waited for: 5 -> 0; matrix products, arithmetic and copies ran while one was open for 13% -> 0% of each run, Pallas kernels for 0% -> 0%
where the time goes in v1:
time: 89.6 us; the launch traced here: 89.4 us
  Pallas kernels  82.4 us (92%)
  between operations  3.75 us (4%)
  other arithmetic  3.18 us (4%)
    pallas_call x1, Pallas kernels, gather_body(): pl.pallas_call(functools.partial(exchange_kernel, n, groups, rounds, edge...  82.4 us
    mul x1, other arithmetic, gather_body(): return (logit_scale * image_grad, logit_scale * text_grad, loss.reshape(()))  3.18 us

profile of v1, /device:TPU:0, one launch (start us, length us, event | category | flops | bytes accessed | tf_op | source)
XLA Modules:
  0.0 89.4 jit_solution(6477412425789686052)
XLA Ops:
  1.9 82.4 %shard_map.85 = (f32[1,256,1152]{2,1,0:T(8,128)}, f32[1,256,1152]{2,1,0:T(8,128)}, f32[1,1]{1,0:T(1,128)}) custom-call(s32[2,8]{1,0:T(2,128)} %partners_ref.1, f32[1]{0:T(128)} %bitcast.3.scale_ref, f32[1]{0:T(128)} %bitcast.4.bias_ref, s32[1,1,256]{2,1,0:T(1,128)} %labels_ref.1, bf16[1,256,1152]{2,1,0:T(8,128)(2,1)} %images_ref.1, ...), custom_call_target="tpu_custom_call" | custom-call | tf_op jit(solution)/shard_map/pallas_call | solution.py:308
  84.3 3.2 %broadcast_multiply_fusion = (f32[1,256,1152]{2,1,0:T(8,128)}, f32[1,256,1152]{2,1,0:T(8,128)}) fusion(f32[1,256,1152]{2,1,0:T(8,128)} %get-tuple-element.7, f32[]{:T(128)} %copy.10, f32[1,256,1152]{2,1,0:T(8,128)} %get-tuple-element.6), kind=kLoop, calls=%fused_computation | loop fusion | flops 589824 | bytes 4718596 | tf_op jit(solution)/shard_map/mul | solution.py:334

commit v2 on v1

--- a/solution.py
+++ b/solution.py
@@ -101,7 +101,7 @@
     n, groups, rounds, edges,
     partners_ref, scale_ref, bias_ref, labels_ref, images_ref, texts_ref,
     image_acc, text_acc, loss_ref,
-    own, loss_sum, group_loss, block_loss,
+    own, end_images, loss_sum, group_loss, block_loss,
     own_sem, load_sem, recv_sem, send_sem, slot_sem,
     group_send, group_recv, block_send, block_recv, *buffers,
 ):
@@ -210,6 +210,9 @@
 
         pl.when(outer)(lambda: slot_copy(k).wait_recv())
 
+    def add_loss(terms):
+        loss_sum[...] += fold(terms)
+
     def compute(k):
         found = [
             held[k][jnp.where(inner, partners_ref[r, me], n + r)] for r in range(rounds)
@@ -217,7 +220,7 @@
         their_images = jnp.concatenate([rows[0] for rows in found], axis=0)
         their_texts = jnp.concatenate([rows[1] for rows in found], axis=0)
         weight, terms = logistic_terms(scale * rows_dot(their_texts, own[0]) + bias)
-        loss_sum[...] += fold(terms)
+        pl.when(inner)(lambda: add_loss(terms))
         mirror, _ = logistic_terms(scale * rows_dot(their_images, own[1]) + bias)
         image_acc[0] += weight_dot(weight.astype(jnp.bfloat16), their_texts)
         text_acc[0] += weight_dot(mirror.astype(jnp.bfloat16), their_images)
@@ -228,61 +231,87 @@
             copy.wait()
         send_own(k, always if k < 2 else outer)
 
-    for copy in own_loads:
-        copy.wait()
-    logits = scale * rows_dot(own[1], own[0]) + bias
-    positive = lax.broadcasted_iota(jnp.int32, logits.shape, 0) == labels_ref[0]
-    signed = jnp.where(positive, -1.0, 1.0)
-    weight, terms = logistic_terms(signed * logits)
-    weight = (signed * weight).astype(jnp.bfloat16)
-    loss_sum[...] = fold(terms)
-    image_acc[0] = weight_dot(weight, own[1])
-    text_acc[0] = jnp.dot(weight, own[0], preferred_element_type=jnp.float32)
-
-    relay(0, True)
-    for k in range(chunks):
-        if k + 1 < chunks:
-            relay(k + 1, True)
-        if k + 2 < chunks:
-            send_own(k + 2, inner)
-        relay(k, False)
-        select(k)
-        compute(k)
+    def own_pair():
+        logits = scale * rows_dot(own[1], own[0]) + bias
+        positive = lax.broadcasted_iota(jnp.int32, logits.shape, 0) == labels_ref[0]
+        signed = jnp.where(positive, -1.0, 1.0)
+        weight, terms = logistic_terms(signed * logits)
+        weight = (signed * weight).astype(jnp.bfloat16)
+        loss_sum[...] = fold(terms)
+        image_acc[0] = weight_dot(weight, own[1])
+        text_acc[0] = jnp.dot(weight, own[0], preferred_element_type=jnp.float32)
+
+    def end_rows():
+        for k in range(chunks):
+            end_images[edges[k] : edges[k + 1]] = held[k][end_device, 0]
+
+    def end_loss(k):
+        texts = jnp.concatenate([slots[k][r, 1] for r in range(rounds)], axis=0)
+        _, terms = logistic_terms(scale * rows_dot(texts, end_images[...]) + bias)
+        loss_sum[...] += fold(terms)
 
     def share(slot, position, count, axis, send, recv):
-        def copy(step):
+        def copy(step, index):
             return pltpu.make_async_remote_copy(
-                src_ref=slot.at[position],
-                dst_ref=slot.at[position],
+                src_ref=slot.at[index],
+                dst_ref=slot.at[index],
                 send_sem=send.at[step],
-                recv_sem=recv.at[position],
+                recv_sem=recv.at[index],
                 device_id={axis: lax.rem(position + step, count)},
                 device_id_type=MESH,
             )
 
-        for step in range(1, count):
-            copy(step).start()
-        for step in range(1, count):
-            other = lax.rem(position + step, count)
-            pltpu.make_async_remote_copy(
-                src_ref=slot.at[other],
-                dst_ref=slot.at[other],
-                send_sem=send.at[step],
-                recv_sem=recv.at[other],
-                device_id={axis: other},
-                device_id_type=MESH,
-            ).wait_recv()
-        for step in range(1, count):
-            copy(step).wait_send()
-        total = slot[0]
-        for at in range(1, count):
-            total = total + slot[at]
-        return total
-
-    group_loss[grp] = loss_sum[...]
-    block_loss[me] = share(group_loss, grp, groups, "grp", group_send, group_recv)
-    total = share(block_loss, me, n, "blk", block_send, block_recv)
-    loss_ref[0, 0] = jnp.sum(total) / jnp.float32(n * groups * own.shape[1])
+        def start():
+            for step in range(1, count):
+                copy(step, position).start()
+
+        def finish():
+            for step in range(1, count):
+                copy(step, lax.rem(position + step, count)).wait_recv()
+            for step in range(1, count):
+                copy(step, position).wait_send()
+            total = slot[0]
+            for at in range(1, count):
+                total = total + slot[at]
+            return total
+
+        return start, finish
+
+    group_start, group_finish = share(group_loss, grp, groups, "grp", group_send, group_recv)
+    block_start, block_finish = share(block_loss, me, n, "blk", block_send, block_recv)
+
+    def send_loss():
+        group_loss[grp] = loss_sum[...]
+        group_start()
+        block_loss[me] = group_finish()
+        block_start()
+
+    for copy in own_loads:
+        copy.wait()
+    half = chunks // 2
+    ahead = 0
+    for k in range(chunks):
+        while ahead < min(2 * k + 2, chunks):
+            relay(ahead, True)
+            if 0 < ahead < chunks - 1:
+                send_own(ahead + 1, inner)
+            ahead += 1
+        if k == 0:
+            pl.when(outer)(own_pair)
+            pl.when(outer)(send_loss)
+        relay(k, False)
+        select(k)
+        if k == 0:
+            pl.when(inner)(own_pair)
+        compute(k)
+        if k == half:
+            pl.when(beside_end)(end_rows)
+        if k >= half:
+            for j in (2 * (k - half), 2 * (k - half) + 1):
+                if j < chunks:
+                    pl.when(beside_end)(functools.partial(end_loss, j))
+    pl.when(inner)(send_loss)
+    loss_ref[0, 0] = jnp.sum(block_finish()) / jnp.float32(n * groups * own.shape[1])
 
     for when, wait in pending:
         pl.when(when)(wait)
@@ -291,7 +320,8 @@
 
 
 def chunk_edges(rows):
-    return list(range(0, rows, CHUNK_ROWS)) + [rows]
+    half = CHUNK_ROWS // 2
+    return [0] + list(range(half, rows, CHUNK_ROWS)) + [rows]
 
 
 def gather_body(n, groups, images, texts, labels, partners, logit_scale, logit_bias):
@@ -312,6 +342,7 @@
         out_specs=(vmem, vmem, smem),
         scratch_shapes=[
             pltpu.VMEM((2, rows, width), images.dtype),
+            pltpu.VMEM((rows, width), images.dtype),
             pltpu.VMEM((8, 128), jnp.float32),
             pltpu.VMEM((groups, 8, 128), jnp.float32),
             pltpu.VMEM((n, 8, 128), jnp.float32),

time: 89.6 us -> 82.3 us (0.919)
  Pallas kernels: 82.4 us -> 75.1 us
    pallas_call x1, Pallas kernels: 82.4 us -> 75.1 us  [gather_body(): pl.pallas_call(functools.partial(exchange_kernel, n, groups, rounds, edge...]
where the time goes in v2:
time: 82.3 us; the launch traced here: 82.1 us
  Pallas kernels  75.1 us (91%)
  between operations  3.75 us (5%)
  other arithmetic  3.18 us (4%)
    pallas_call x1, Pallas kernels, gather_body(): pl.pallas_call(functools.partial(exchange_kernel, n, groups, rounds, edge...  75.1 us
    mul x1, other arithmetic, gather_body(): return (logit_scale * image_grad, logit_scale * text_grad, loss.reshape(()))  3.18 us

profile of v2, /device:TPU:0, one launch (start us, length us, event | category | flops | bytes accessed | tf_op | source)
XLA Modules:
  0.0 82.1 jit_solution(7474794293777177714)
XLA Ops:
  1.9 75.1 %shard_map.85 = (f32[1,256,1152]{2,1,0:T(8,128)}, f32[1,256,1152]{2,1,0:T(8,128)}, f32[1,1]{1,0:T(1,128)}) custom-call(s32[2,8]{1,0:T(2,128)} %partners_ref.1, f32[1]{0:T(128)} %bitcast.3.scale_ref, f32[1]{0:T(128)} %bitcast.4.bias_ref, s32[1,1,256]{2,1,0:T(1,128)} %labels_ref.1, bf16[1,256,1152]{2,1,0:T(8,128)(2,1)} %images_ref.1, ...), custom_call_target="tpu_custom_call" | custom-call | tf_op jit(solution)/shard_map/pallas_call | solution.py:338
  77.1 3.2 %broadcast_multiply_fusion = (f32[1,256,1152]{2,1,0:T(8,128)}, f32[1,256,1152]{2,1,0:T(8,128)}) fusion(f32[1,256,1152]{2,1,0:T(8,128)} %get-tuple-element.7, f32[]{:T(128)} %copy.10, f32[1,256,1152]{2,1,0:T(8,128)} %get-tuple-element.6), kind=kLoop, calls=%fused_computation | loop fusion | flops 589824 | bytes 4718596 | tf_op jit(solution)/shard_map/mul | solution.py:365
